TPU v7x, 32 devices: a whole 2x2x4 slice. The times are simulated.
32 devices in a mesh: section: 2 (over x), dp: 16 (over z, y, core).
Axes of the slice: x: 2, y: 2, z: 4, core: 2. Of those that a mesh axis runs over, the one named last changes fastest.
Arguments:
- activations: bfloat16 [4, 256, 4608], P('section', 'dp'), may hold values from -6 to 6
- section_sources: int32 [4], replicated, may hold values from 0 to 3, as said below
- accumulators: float32 [256, 4, 4608], P('dp', 'section'), may hold values from -6 to 6
- block_sources: int32 [256], replicated, may hold values from 0 to 255, as said below
- loss_terms: float32 [2, 16], P('section', 'dp'), may hold values from 0.35 to 6
- pre_gain: float32 [2, 4608], P('section'), may hold values from 0.1 to 1.9
- query_weight: bfloat16 [2, 4608, 2048], P('section', None, 'dp'), may hold values from -0.09375 to 0.09375
- keyval_weight: bfloat16 [2, 4608, 2048], P('section', None, 'dp'), may hold values from -0.09375 to 0.09375
- output_weight: bfloat16 [2, 2048, 4608], P('section', 'dp'), may hold values from -0.125 to 0.125
- post_gain: float32 [2, 4608], P('section'), may hold values from 0.1 to 1.9
Outputs:
- new_activations: bfloat16 [4, 256, 4608], P('section', 'dp')
- new_accumulators: float32 [256, 4, 4608], P('dp', 'section')
- check_out: bfloat16 [2, 256, 4608], P('section', 'dp')
Inputs may be any that keep to these rules, and one draw needn't show every extreme that they name: `section_sources`: A permutation; each old section's micro-batches fill 1 slots of each new section. `block_sources`: A permutation; each old data index's blocks fill 1 block of each new data index.
All inputs are finite; a program needn't handle non-finite values.
Results may differ from a plain program's by a relative error of at most 0.014.
Values may be sent and summed in bfloat16 or wider, within the bound.
A program may use at most 64 MiB of HBM per device.

v0:
```python
import jax
import jax.numpy as jnp
from jax import lax
from jax.sharding import PartitionSpec as P

D = 4608


def partner(value, axis, stride):
    mask = 2**stride
    pairs = [(source, source ^ mask) for source in range(lax.axis_size(axis))]
    return lax.ppermute(value, axis, pairs)


def rms_norm(values, gain):
    meansq = jnp.mean(values * values, axis=-1, keepdims=True)
    return values * lax.rsqrt(meansq + 1e-06) * gain


def rotary(values, positions):
    width = values.shape[-1]
    middle = width // 2
    counter = jnp.arange(middle, dtype=jnp.float32)
    freqs = 10000.0 ** (-2.0 * counter / width)
    angles = positions.astype(jnp.float32)[:, None] * freqs[None, :]
    cosine = jnp.cos(angles)
    sine = jnp.sin(angles)
    first = values[..., :middle]
    second = values[..., middle:]
    return jnp.concatenate(
        [first * cosine - second * sine, second * cosine + first * sine], axis=-1
    )


def plan_routes(sources, own_index, groups, per_group):
    per_peer = per_group // groups
    table = sources.reshape(groups, per_group)
    owners = table // per_group
    places = table % per_group
    slot_ids = jnp.arange(per_group, dtype=jnp.int32)
    sort_keys = jnp.where(owners == own_index, slot_ids[None, :], slot_ids[None, :] + per_group)
    ranking = jnp.argsort(sort_keys, axis=1)[:, :per_peer]
    send_index = jnp.take_along_axis(places, ranking, axis=1).reshape(-1)
    my_owners = lax.dynamic_slice_in_dim(owners, own_index, 1, 0)[0]
    earlier = (my_owners[None, :] == my_owners[:, None]) & (slot_ids[None, :] < slot_ids[:, None])
    earlier_count = jnp.sum(earlier.astype(jnp.int32), axis=1)
    recv_index = my_owners * per_peer + earlier_count
    return (send_index, recv_index)


def on_device(
    activations,
    section_sources,
    accumulators,
    block_sources,
    loss_terms,
    pre_gain,
    query_weight,
    keyval_weight,
    output_weight,
    post_gain,
):
    section_index = lax.axis_index("section")
    mb_local = activations.shape[0]
    gathered = lax.all_gather(activations, "section", axis=0, tiled=True)
    my_slots = lax.dynamic_slice_in_dim(section_sources, section_index * mb_local, mb_local)
    moved = jnp.take(gathered, my_slots, axis=0)
    data_ranks = lax.axis_size("dp")
    data_index = lax.axis_index("dp")
    blk_local = accumulators.shape[0]
    per_peer = blk_local // data_ranks
    block_send, block_recv = plan_routes(block_sources, data_index, data_ranks, blk_local)
    outgoing_blocks = jnp.take(accumulators, block_send, axis=0)
    term_rows = jnp.broadcast_to(loss_terms, (blk_local, 1))
    incoming_blocks, incoming_terms = (
        lax.all_to_all(
            outgoing_blocks.astype(jnp.bfloat16), "dp", split_axis=0, concat_axis=0, tiled=True
        ).astype(outgoing_blocks.dtype),
        lax.all_to_all(
            term_rows.astype(jnp.bfloat16), "dp", split_axis=0, concat_axis=0, tiled=True
        ).astype(term_rows.dtype),
    )
    scale_sum = jnp.sum(incoming_terms[::per_peer, 0])
    factor = data_ranks / scale_sum
    new_accumulators = jnp.take(incoming_blocks, block_recv, axis=0) * factor
    checked = moved[0]
    head_size = query_weight.shape[2]
    is_even = data_index % 2 == 0
    w_query = query_weight[0]
    w_keyval = keyval_weight[0]
    gain_pre = pre_gain[0]
    block_rows = lax.all_gather(checked, "dp", axis=0, tiled=True)
    row_count = block_rows.shape[0]
    positions = jnp.arange(row_count, dtype=jnp.int32)
    normed = rms_norm(block_rows.astype(jnp.float32), gain_pre).astype(jnp.bfloat16)
    queries = jnp.dot(normed, w_query, preferred_element_type=jnp.float32)
    own_proj = jnp.dot(normed, w_keyval, preferred_element_type=jnp.float32)
    queries = rotary(queries, positions)
    own_proj = jnp.where(is_even, rotary(own_proj, positions), own_proj)
    projected = jnp.concatenate([queries, own_proj], axis=1).astype(jnp.bfloat16)
    queries = projected[:, :head_size]
    own_kv = projected[:, head_size:]
    partner_kv = partner(own_kv, "dp", 0)
    key_rows = jnp.where(is_even, own_kv, partner_kv)
    value_rows = jnp.where(is_even, partner_kv, own_kv)
    length = projected.shape[0]
    positions = jnp.arange(length, dtype=jnp.int32)
    scale_factor = (D / data_ranks) ** (-0.5)
    scores = (
        lax.dot_general(
            queries, key_rows, (((1,), (1,)), ((), ())), preferred_element_type=jnp.float32
        )
        * scale_factor
    )
    capped = 50.0 * jnp.tanh(scores / 50.0)
    causal = positions[None, :] <= positions[:, None]
    expd = jnp.where(causal, jnp.exp(capped), 0.0)
    denominator = jnp.sum(expd, axis=-1, keepdims=True)
    probs = expd.astype(jnp.bfloat16)
    numer = jnp.dot(probs, value_rows, preferred_element_type=jnp.float32)
    attended = (numer / denominator).astype(jnp.bfloat16)
    w_output = output_weight[0]
    summed = lax.psum_scatter(
        jnp.dot(attended, w_output, preferred_element_type=jnp.float32).astype(jnp.bfloat16),
        "dp",
        scatter_dimension=0,
        tiled=True,
    ).astype(jnp.float32)
    check_out = (checked.astype(jnp.float32) + rms_norm(summed, post_gain[0])).astype(jnp.bfloat16)
    return (moved, new_accumulators, check_out[None, :, :])


def solution(mesh):
    placed = (
        P("section", "dp", None),
        P(),
        P("dp", "section", None),
        P(),
        P("section", "dp"),
        P("section", None),
        P("section", None, "dp"),
        P("section", None, "dp"),
        P("section", "dp", None),
        P("section", None),
    )
    return jax.shard_map(
        on_device,
        mesh=mesh,
        in_specs=placed,
        out_specs=(P("section", "dp", None), P("dp", "section", None), P("section", "dp", None)),
        check_vma=False,
    )
```

profile of v0, /device:TPU:0, one launch (start us, length us, event | category | flops | bytes accessed | tf_op | source)
XLA Modules:
  0.0 145.7 jit_solution(12692090813205101284)
XLA Ops:
  7.3 0.8 compare_and_fusion.2
  8.1 10.9 %all_gather.6 = bf16[4,16,4608]{2,1,0:T(8,128)(2,1)S(1)} all-gather(bf16[2,16,4608]{2,1,0:T(8,128)(2,1)} %param.12), channel_id=1, replica_groups=mesh['section'=2,'dp'=16] {'section'}, dimensions={0}, use_global_device_ids=true | all-gather | bytes 884736 | tf_op jit(solution)/shard_map/all_gather | solution.py:65
  19.0 0.6 gather_fusion
  19.6 0.1 broadcast_select_fusion
  19.7 0.7 slice.38
  21.1 0.6 broadcast_in_dim.70
  21.7 6.1 %all-to-all-start.1 = ((bf16[16,1,1]{2,1,0:T(2,128)(2,1)}), bf16[16,1,1]{2,1,0:T(2,128)(2,1)S(1)}, u32[]{:S(2)}, u32[]{:S(2)}) async-start(bf16[16,1,1]{2,1,0:T(2,128)(2,1)} %broadcast_in_dim.70), calls=%async_computation.1 | async-start | bytes 16384 | tf_op jit(solution)/shard_map/all_to_all | solution.py:79
  28.1 0.7 sort.17
  28.9 35.5 %all-gather.3.cloned.1.call-done = bf16[1,256,4608]{2,1,0:T(8,128)(2,1)} async-done(((bf16[1,16,4608]{2,1,0:T(8,128)(2,1)}), bf16[1,256,4608]{2,1,0:T(8,128)(2,1)}) %all-gather.3.cloned.1.call-update) | async-done | bytes 2359312 | tf_op jit(solution)/shard_map/all_gather | solution.py:92
  64.4 2.4 %fusion = f32[256]{0:T(256)S(1)} fusion(bf16[1,256,4608]{2,1,0:T(8,128)(2,1)} %all-gather.3.cloned.1.call-done), kind=kLoop, calls=%fused_computation.7 | loop fusion | flops 3538688 | bytes 2360320 | tf_op jit(solution)/shard_map/reduce_sum | solution.py:16
  66.8 2.4 %fusion.4 = f32[256,128]{0,1:T(8,128)S(1)} fusion(bf16[1,4608,128]{2,1,0:T(8,128)(2,1)} %param.19, bf16[1,256,4608]{2,1,0:T(8,128)(2,1)S(1)} %copy-done.1, f32[4608]{0:T(1024)S(1)} %reduce.1, f32[256]{0:T(256)S(1)} %add_rsqrt_fusion), kind=kOutput, calls=%fused_computation.11 | convolution fusion | flops 306708480 | bytes 3689472 | tf_op jit(solution)/shard_map/dot_general | solution.py:97
  69.2 0.3 fusion.35
  69.5 0.3 collective-permute-start
  69.8 1.1 fusion.6
  70.9 0.3 fusion.32
  71.3 0.3 fusion.52
  71.6 2.4 %convolution_convert_fusion = bf16[256,4608]{1,0:T(8,128)(2,1)} fusion(bf16[1,128,4608]{2,1,0:T(8,128)(2,1)S(1)} %copy-done, bf16[256,256]{0,1:T(8,128)(2,1)S(1)} %get-tuple-element.20, f32[256]{0:T(256)S(1)} %get-tuple-element.19, bf16[256,128]{0,1:T(8,128)(2,1)S(1)} %collective-permute-done, bf16[256,128]{0,1:T(8,128)(2,1)S(1)} %fusion.20, pred[]{:T(512)S(6)} %eq.31), kind=kOutput, calls=%fused_computation.4 | convolution fusion | flops 320045056 | bytes 3802113 | tf_op jit(solution)/shard_map/dot_general | solution.py:124
  74.0 0.7 gather_fusion.1
  74.7 0.3 copy-done.3
  75.0 1.2 gather_fusion.2
  76.2 1.0 select_convert_fusion
  77.3 3.6 %all-to-all-start = ((bf16[16,2,4608]{2,1,0:T(2,128)(2,1)}), bf16[16,2,4608]{2,1,0:T(2,128)(2,1)S(1)}, u32[]{:S(2)}, u32[]{:S(2)}) async-start(bf16[16,2,4608]{2,1,0:T(2,128)(2,1)} %select_convert_fusion), calls=%async_computation | async-start | bytes 589824 | tf_op jit(solution)/shard_map/all_to_all | solution.py:76
  80.9 0.2 convert_reduce_fusion
  81.1 0.1 copy.19
  81.2 0.6 convert_reduce_fusion.1
  82.5 8.9 %all-to-all-done = bf16[16,2,4608]{2,1,0:T(2,128)(2,1)S(1)} async-done(((bf16[16,2,4608]{2,1,0:T(2,128)(2,1)}), bf16[16,2,4608]{2,1,0:T(2,128)(2,1)S(1)}, u32[]{:S(2)}, u32[]{:S(2)}) %all-to-all-start) | async-done | bytes 294944 | tf_op jit(solution)/shard_map/all_to_all | solution.py:76
  91.4 0.2 convert_element_type.71
  91.6 1.2 gather_fusion.3
  92.8 1.1 select_multiply_fusion
  93.9 42.2 %reduce-scatter.2.cloned.1.call-done = bf16[16,4608]{1,0:T(8,128)(2,1)} async-done(((bf16[256,4608]{1,0:T(8,128)(2,1)}), bf16[16,4608]{1,0:T(8,128)(2,1)}) %reduce-scatter.2.cloned.1.call-update) | async-done | bytes 147472 | tf_op jit(solution)/shard_map/reduce_scatter | solution.py:123
  136.1 1.1 fusion.15
  137.1 1.7 %fusion.19 = bf16[1,16,4608]{2,1,0:T(8,128)(2,1)} fusion(bf16[16,4608]{1,0:T(8,128)(2,1)} %reduce-scatter.2.cloned.1.call-done, f32[4608]{0:T(1024)S(1)} %reduce.2, f32[16]{0:T(128)S(1)} %add_rsqrt_fusion.1, bf16[2,16,4608]{2,1,0:T(8,128)(2,1)S(1)} %broadcast_select_fusion), kind=kLoop, calls=%fused_computation.32 | loop fusion | flops 442368 | bytes 460864 | tf_op jit(solution)/shard_map/broadcast_in_dim | solution.py:130
  (43 shorter events, 0.6 us)
Async XLA Ops:
  7.2 64.4 %copy-start = (bf16[1,128,4608]{2,1,0:T(8,128)(2,1)S(1)}, bf16[1,128,4608]{2,1,0:T(8,128)(2,1)}, u32[]{:S(2)}) copy-start(bf16[1,128,4608]{2,1,0:T(8,128)(2,1)} %param.20) | copy-start | bytes 3538948
  7.2 20.7 %copy-start.6 = (s32[256]{0:T(256)S(1)}, s32[256]{0:T(256)}, u32[]{:S(2)}) copy-start(s32[256]{0:T(256)} %param.15) | copy-start | bytes 3076
  7.2 20.9 %copy-start.4 = (f32[1,4608]{1,0:T(1,128)S(1)}, f32[1,4608]{1,0:T(1,128)}, u32[]{:S(2)}) copy-start(f32[1,4608]{1,0:T(1,128)} %param.17) | copy-start | bytes 55300
  7.2 57.2 %all-gather.3.cloned.1.call-start = ((), (), s32[]{:S(2)}) async-start(), calls=%async_computation.4 | async-start | bytes 2506752 | tf_op jit(solution)/shard_map/all_gather | solution.py:92
  19.7 117.5 %copy-start.2 = (bf16[2,16,4608]{2,1,0:T(8,128)(2,1)}, bf16[2,16,4608]{2,1,0:T(8,128)(2,1)S(1)}, u32[]{:S(2)}) copy-start(bf16[2,16,4608]{2,1,0:T(8,128)(2,1)S(1)} %broadcast_select_fusion) | copy-start | bytes 884740
  21.7 55.6 %all-to-all-start.1 = ((bf16[16,1,1]{2,1,0:T(2,128)(2,1)}), bf16[16,1,1]{2,1,0:T(2,128)(2,1)S(1)}, u32[]{:S(2)}, u32[]{:S(2)}) async-start(bf16[16,1,1]{2,1,0:T(2,128)(2,1)} %broadcast_in_dim.70), calls=%async_computation.1 | async-start | bytes 16384 | tf_op jit(solution)/shard_map/all_to_all | solution.py:79
  27.8 108.3 %reduce-scatter.2.cloned.1.call-start = ((), (), s32[]{:S(2)}) async-start(), calls=%async_computation.3 | async-start | bytes 2506752 | tf_op jit(solution)/shard_map/reduce_scatter | solution.py:123
  64.4 2.4 %copy-start.1 = (bf16[1,256,4608]{2,1,0:T(8,128)(2,1)S(1)}, bf16[1,256,4608]{2,1,0:T(8,128)(2,1)}, u32[]{:S(2)}) copy-start(bf16[1,256,4608]{2,1,0:T(8,128)(2,1)} %all-gather.3.cloned.1.call-done) | copy-start | bytes 7077892
  66.8 3.1 %copy-start.7 = (bf16[1,4608,128]{2,1,0:T(8,128)(2,1)S(1)}, bf16[1,4608,128]{2,1,0:T(8,128)(2,1)}, u32[]{:S(2)}) copy-start(bf16[1,4608,128]{2,1,0:T(8,128)(2,1)} %param.18) | copy-start | bytes 3538948
  69.5 1.7 %collective-permute-start = (bf16[256,128]{0,1:T(8,128)(2,1)S(1)}, bf16[256,128]{0,1:T(8,128)(2,1)S(1)}, u32[]{:S(2)}, u32[]{:S(2)}) collective-permute-start(bf16[256,128]{0,1:T(8,128)(2,1)S(1)} %fusion.20), channel_id=1, source_target_pairs={{0,1},{1,0},{2,3},{3,2},{4,5},{5,4},{6,7},{7,6},{8,9},{9,8},{10,11... | collective-permute-start | bytes 196616 | tf_op jit(solution)/shard_map/ppermute | solution.py:12
  74.0 1.1 copy-start.3
  74.0 3.3 %copy-start.5 = (f32[1,4608]{1,0:T(1,128)S(1)}, f32[1,4608]{1,0:T(1,128)}, u32[]{:S(2)}) copy-start(f32[1,4608]{1,0:T(1,128)} %param.21) | copy-start | bytes 55300
  77.3 14.1 %all-to-all-start = ((bf16[16,2,4608]{2,1,0:T(2,128)(2,1)}), bf16[16,2,4608]{2,1,0:T(2,128)(2,1)S(1)}, u32[]{:S(2)}, u32[]{:S(2)}) async-start(bf16[16,2,4608]{2,1,0:T(2,128)(2,1)} %select_convert_fusion), calls=%async_computation | async-start | bytes 589824 | tf_op jit(solution)/shard_map/all_to_all | solution.py:76
Sparse Core Ops, SparseCore 0:
  20.5 43.7 all-gather.2
  74.1 61.9 reduce-scatter.1
where the time goes:
time: 146 us
  waiting for transfers between devices  86.6 us (59%)
  between operations  15.7 us (11%)
  blocking collectives  10.9 us (7%)
  other arithmetic  10.8 us (7%)
  starting transfers between devices  10.1 us (7%)
  matrix products  6.18 us (4%)
  local copies, waits for them, and re-layouts  5.5 us (4%)
    reduce_scatter x1, waiting for transfers between devices, on_device(): lax.psum_scatter(jnp.dot(attended, w_output, preferred_element_type=jnp.f...  42.2 us
    all_gather x1, waiting for transfers between devices, on_device(): block_rows = lax.all_gather(checked, 'dp', axis=0, tiled=True)  35.5 us
    all_gather x1, blocking collectives, on_device(): gathered = lax.all_gather(activations, 'section', axis=0, tiled=True)  10.9 us
    all_to_all x1, waiting for transfers between devices, on_device(): lax.all_to_all(outgoing_blocks.astype(jnp.bfloat16), 'dp', split_axis=0,...  8.9 us
    all_to_all x1, starting transfers between devices, on_device(): lax.all_to_all(term_rows.astype(jnp.bfloat16), 'dp', split_axis=0, concat...  6.13 us
    all_to_all x1, starting transfers between devices, on_device(): lax.all_to_all(outgoing_blocks.astype(jnp.bfloat16), 'dp', split_axis=0,...  3.55 us
    reduce_sum x2, other arithmetic, rms_norm(): meansq = jnp.mean(values * values, axis=-1, keepdims=True)  3.42 us
  transfers between devices with their start and end apart: 5, of which 3 were waited for; matrix products, arithmetic and copies ran while one was open for 12% of the time, Pallas kernels for 0%

commit v1 on v0

--- a/solution.py
+++ b/solution.py
@@ -89,7 +89,12 @@
     w_query = query_weight[0]
     w_keyval = keyval_weight[0]
     gain_pre = pre_gain[0]
-    block_rows = lax.all_gather(checked, "dp", axis=0, tiled=True)
+    ring = [checked]
+    for hop in range(15):
+        ring.append(lax.ppermute(ring[-1], "dp", [(dev, (dev + 1) % 16) for dev in range(16)]))
+    block_rows = jnp.roll(
+        jnp.concatenate(ring[::-1], axis=0), (lax.axis_index("dp") + 1) * ring[0].shape[0], axis=0
+    )
     row_count = block_rows.shape[0]
     positions = jnp.arange(row_count, dtype=jnp.int32)
     normed = rms_norm(block_rows.astype(jnp.float32), gain_pre).astype(jnp.bfloat16)

time: 146 us -> 210 us (1.44)
  waiting for transfers between devices: 86.6 us -> 146 us
  other arithmetic: 10.8 us -> 14.1 us
  local copies, waits for them, and re-layouts: 5.5 us -> 8.15 us
    ppermute x0 -> x15, waiting for transfers between devices: none -> 96.8 us  [on_device(): lax.ppermute(ring[-1], 'dp', [(dev, (dev + 1) % 16) for dev in range(16)])]
    all_gather x1 -> x0, waiting for transfers between devices: 35.5 us -> none  [on_device(): block_rows = lax.all_gather(checked, 'dp', axis=0, tiled=True)]
    reduce_scatter x1, waiting for transfers between devices: 42.2 us -> 39.8 us  [on_device(): lax.psum_scatter(jnp.dot(attended, w_output, preferred_element_type=jnp.f...]
  transfers between devices with their start and end apart: 5 -> 19, of which waited for: 3 -> 17; matrix products, arithmetic and copies ran while one was open for 12% -> 11% of each run, Pallas kernels for 0% -> 0%
where the time goes in v1:
time: 210 us
  waiting for transfers between devices  146 us (70%)
  between operations  15.9 us (8%)
  other arithmetic  14.1 us (7%)
  blocking collectives  10.9 us (5%)
  starting transfers between devices  10 us (5%)
  local copies, waits for them, and re-layouts  8.15 us (4%)
  matrix products  4.83 us (2%)
    ppermute x15, waiting for transfers between devices, on_device(): lax.ppermute(ring[-1], 'dp', [(dev, (dev + 1) % 16) for dev in range(16)])  96.8 us
    reduce_scatter x1, waiting for transfers between devices, on_device(): lax.psum_scatter(jnp.dot(attended, w_output, preferred_element_type=jnp.f...  39.8 us
    all_gather x1, blocking collectives, on_device(): gathered = lax.all_gather(activations, 'section', axis=0, tiled=True)  10.9 us
    all_to_all x1, waiting for transfers between devices, on_device(): lax.all_to_all(outgoing_blocks.astype(jnp.bfloat16), 'dp', split_axis=0,...  8.23 us
    all_to_all x1, starting transfers between devices, on_device(): lax.all_to_all(term_rows.astype(jnp.bfloat16), 'dp', split_axis=0, concat...  5.82 us
  transfers between devices with their start and end apart: 19, of which 17 were waited for; matrix products, arithmetic and copies ran while one was open for 11% of the time, Pallas kernels for 0%

profile of v1, /device:TPU:0, one launch (start us, length us, event | category | flops | bytes accessed | tf_op | source)
XLA Modules:
  0.0 209.7 jit_solution(3228997681981851938)
XLA Ops:
  8.0 10.9 %all_gather.3 = bf16[4,16,4608]{2,1,0:T(8,128)(2,1)S(1)} all-gather(bf16[2,16,4608]{2,1,0:T(8,128)(2,1)} %param.12), channel_id=1, replica_groups=mesh['section'=2,'dp'=16] {'section'}, dimensions={0}, use_global_device_ids=true | all-gather | bytes 884736 | tf_op jit(solution)/shard_map/all_gather | solution.py:65
  19.7 7.3 %collective-permute-done = bf16[16,4608]{1,0:T(8,128)(2,1)S(1)} collective-permute-done((bf16[16,4608]{1,0:T(8,128)(2,1)S(1)}, bf16[16,4608]{1,0:T(8,128)(2,1)S(1)}, u32[]{:S(2)}, u32[]{:S(2)}) %collective-permute-start) | collective-permute-done | bytes 147488 | tf_op jit(solution)/shard_map/ppermute | solution.py:94
  27.0 7.3 %collective-permute-done.1 = bf16[16,4608]{1,0:T(8,128)(2,1)S(1)} collective-permute-done((bf16[16,4608]{1,0:T(8,128)(2,1)S(1)}, bf16[16,4608]{1,0:T(8,128)(2,1)S(1)}, u32[]{:S(2)}, u32[]{:S(2)}) %collective-permute-start.1) | collective-permute-done | bytes 147488 | tf_op jit(solution)/shard_map/ppermute | solution.py:94
  34.2 7.3 %collective-permute-done.2 = bf16[16,4608]{1,0:T(8,128)(2,1)S(1)} collective-permute-done((bf16[16,4608]{1,0:T(8,128)(2,1)S(1)}, bf16[16,4608]{1,0:T(8,128)(2,1)S(1)}, u32[]{:S(2)}, u32[]{:S(2)}) %collective-permute-start.2) | collective-permute-done | bytes 147488 | tf_op jit(solution)/shard_map/ppermute | solution.py:94
  41.5 7.3 %collective-permute-done.3 = bf16[16,4608]{1,0:T(8,128)(2,1)S(1)} collective-permute-done((bf16[16,4608]{1,0:T(8,128)(2,1)S(1)}, bf16[16,4608]{1,0:T(8,128)(2,1)S(1)}, u32[]{:S(2)}, u32[]{:S(2)}) %collective-permute-start.3) | collective-permute-done | bytes 147488 | tf_op jit(solution)/shard_map/ppermute | solution.py:94
  48.8 7.3 %collective-permute-done.4 = bf16[16,4608]{1,0:T(8,128)(2,1)S(1)} collective-permute-done((bf16[16,4608]{1,0:T(8,128)(2,1)S(1)}, bf16[16,4608]{1,0:T(8,128)(2,1)S(1)}, u32[]{:S(2)}, u32[]{:S(2)}) %collective-permute-start.4) | collective-permute-done | bytes 147488 | tf_op jit(solution)/shard_map/ppermute | solution.py:94
  56.0 7.3 %collective-permute-done.5 = bf16[16,4608]{1,0:T(8,128)(2,1)S(1)} collective-permute-done((bf16[16,4608]{1,0:T(8,128)(2,1)S(1)}, bf16[16,4608]{1,0:T(8,128)(2,1)S(1)}, u32[]{:S(2)}, u32[]{:S(2)}) %collective-permute-start.5) | collective-permute-done | bytes 147488 | tf_op jit(solution)/shard_map/ppermute | solution.py:94
  63.3 7.3 %collective-permute-done.6 = bf16[16,4608]{1,0:T(8,128)(2,1)S(1)} collective-permute-done((bf16[16,4608]{1,0:T(8,128)(2,1)S(1)}, bf16[16,4608]{1,0:T(8,128)(2,1)S(1)}, u32[]{:S(2)}, u32[]{:S(2)}) %collective-permute-start.6) | collective-permute-done | bytes 147488 | tf_op jit(solution)/shard_map/ppermute | solution.py:94
  70.5 7.3 %collective-permute-done.7 = bf16[16,4608]{1,0:T(8,128)(2,1)S(1)} collective-permute-done((bf16[16,4608]{1,0:T(8,128)(2,1)S(1)}, bf16[16,4608]{1,0:T(8,128)(2,1)S(1)}, u32[]{:S(2)}, u32[]{:S(2)}) %collective-permute-start.7) | collective-permute-done | bytes 147488 | tf_op jit(solution)/shard_map/ppermute | solution.py:94
  77.8 7.3 %collective-permute-done.8 = bf16[16,4608]{1,0:T(8,128)(2,1)S(1)} collective-permute-done((bf16[16,4608]{1,0:T(8,128)(2,1)S(1)}, bf16[16,4608]{1,0:T(8,128)(2,1)S(1)}, u32[]{:S(2)}, u32[]{:S(2)}) %collective-permute-start.8) | collective-permute-done | bytes 147488 | tf_op jit(solution)/shard_map/ppermute | solution.py:94
  85.1 7.3 %collective-permute-done.9 = bf16[16,4608]{1,0:T(8,128)(2,1)S(1)} collective-permute-done((bf16[16,4608]{1,0:T(8,128)(2,1)S(1)}, bf16[16,4608]{1,0:T(8,128)(2,1)S(1)}, u32[]{:S(2)}, u32[]{:S(2)}) %collective-permute-start.9) | collective-permute-done | bytes 147488 | tf_op jit(solution)/shard_map/ppermute | solution.py:94
  92.3 7.3 %collective-permute-done.10 = bf16[16,4608]{1,0:T(8,128)(2,1)S(1)} collective-permute-done((bf16[16,4608]{1,0:T(8,128)(2,1)S(1)}, bf16[16,4608]{1,0:T(8,128)(2,1)S(1)}, u32[]{:S(2)}, u32[]{:S(2)}) %collective-permute-start.10) | collective-permute-done | bytes 147488 | tf_op jit(solution)/shard_map/ppermute | solution.py:94
  100.9 5.8 %all-to-all-start.1 = ((bf16[16,1,1]{2,1,0:T(2,128)(2,1)}), bf16[16,1,1]{2,1,0:T(2,128)(2,1)S(1)}, u32[]{:S(2)}, u32[]{:S(2)}) async-start(bf16[16,1,1]{2,1,0:T(2,128)(2,1)} %broadcast_in_dim.70), calls=%async_computation.1 | async-start | bytes 16384 | tf_op jit(solution)/shard_map/all_to_all | solution.py:79
  109.4 5.5 %collective-permute-done.12 = bf16[16,4608]{1,0:T(8,128)(2,1)S(1)} collective-permute-done((bf16[16,4608]{1,0:T(8,128)(2,1)S(1)}, bf16[16,4608]{1,0:T(8,128)(2,1)S(1)}, u32[]{:S(2)}, u32[]{:S(2)}) %collective-permute-start.12) | collective-permute-done | bytes 147488 | tf_op jit(solution)/shard_map/ppermute | solution.py:94
  114.8 1.3 fusion.53
  116.1 6.0 %collective-permute-done.13 = bf16[16,4608]{1,0:T(8,128)(2,1)S(1)} collective-permute-done((bf16[16,4608]{1,0:T(8,128)(2,1)S(1)}, bf16[16,4608]{1,0:T(8,128)(2,1)S(1)}, u32[]{:S(2)}, u32[]{:S(2)}) %collective-permute-start.13) | collective-permute-done | bytes 147488 | tf_op jit(solution)/shard_map/ppermute | solution.py:94
  122.7 1.4 reduce.1
  124.0 5.4 %collective-permute-done.14 = bf16[16,4608]{1,0:T(8,128)(2,1)} collective-permute-done((bf16[16,4608]{1,0:T(8,128)(2,1)S(1)}, bf16[16,4608]{1,0:T(8,128)(2,1)}, u32[]{:S(2)}, u32[]{:S(2)}) %collective-permute-start.14) | collective-permute-done | bytes 147488 | tf_op jit(solution)/shard_map/ppermute | solution.py:94
  129.5 0.9 constant_dynamic-update-slice_fusion.31
  130.7 1.0 constant_dynamic-update-slice_fusion.15
  132.6 1.1 fusion.6
  133.7 1.1 fusion.4
  136.8 2.4 %convolution_convert_fusion = bf16[256,4608]{1,0:T(8,128)(2,1)} fusion(bf16[1,128,4608]{2,1,0:T(8,128)(2,1)S(1)} %copy-done, bf16[256,256]{0,1:T(8,128)(2,1)S(1)} %get-tuple-element.20, f32[256]{0:T(256)S(1)} %get-tuple-element.19, bf16[256,128]{0,1:T(8,128)(2,1)S(1)} %collective-permute-done.15, bf16[256,128]{0,1:T(8,128)(2,1)S(1)} %fusion.20, pred[]{:T(512)S(6)} %eq.34), kind=kOutput, calls=%fused_computation.4 | convolution fusion | flops 320045056 | bytes 3802113 | tf_op jit(solution)/shard_map/dot_general | solution.py:129
  140.7 1.2 gather_fusion.2
  142.5 1.0 select_convert_fusion
  143.6 3.6 %all-to-all-start = ((bf16[16,2,4608]{2,1,0:T(2,128)(2,1)}), bf16[16,2,4608]{2,1,0:T(2,128)(2,1)S(1)}, u32[]{:S(2)}, u32[]{:S(2)}) async-start(bf16[16,2,4608]{2,1,0:T(2,128)(2,1)} %select_convert_fusion), calls=%async_computation | async-start | bytes 589824 | tf_op jit(solution)/shard_map/all_to_all | solution.py:76
  149.5 8.2 %all-to-all-done = bf16[16,2,4608]{2,1,0:T(2,128)(2,1)S(1)} async-done(((bf16[16,2,4608]{2,1,0:T(2,128)(2,1)}), bf16[16,2,4608]{2,1,0:T(2,128)(2,1)S(1)}, u32[]{:S(2)}, u32[]{:S(2)}) %all-to-all-start) | async-done | bytes 294944 | tf_op jit(solution)/shard_map/all_to_all | solution.py:76
  157.9 1.2 gather_fusion.3
  159.1 1.1 select_multiply_fusion
  160.2 39.8 %reduce-scatter.2.cloned.1.call-done = bf16[16,4608]{1,0:T(8,128)(2,1)} async-done(((bf16[256,4608]{1,0:T(8,128)(2,1)}), bf16[16,4608]{1,0:T(8,128)(2,1)}) %reduce-scatter.2.cloned.1.call-update) | async-done | bytes 147472 | tf_op jit(solution)/shard_map/reduce_scatter | solution.py:128
  200.1 1.1 fusion.15
  201.1 1.7 fusion.19
  (104 shorter events, 12.3 us)
Async XLA Ops:
  7.2 129.6 %copy-start = (bf16[1,128,4608]{2,1,0:T(8,128)(2,1)S(1)}, bf16[1,128,4608]{2,1,0:T(8,128)(2,1)}, u32[]{:S(2)}) copy-start(bf16[1,128,4608]{2,1,0:T(8,128)(2,1)} %param.20) | copy-start | bytes 3538948
  19.6 181.5 %copy-start.1 = (bf16[2,16,4608]{2,1,0:T(8,128)(2,1)}, bf16[2,16,4608]{2,1,0:T(8,128)(2,1)S(1)}, u32[]{:S(2)}) copy-start(bf16[2,16,4608]{2,1,0:T(8,128)(2,1)S(1)} %broadcast_select_fusion) | copy-start | bytes 884740
  19.6 7.3 %collective-permute-start = (bf16[16,4608]{1,0:T(8,128)(2,1)S(1)}, bf16[16,4608]{1,0:T(8,128)(2,1)S(1)}, u32[]{:S(2)}, u32[]{:S(2)}) collective-permute-start(bf16[16,4608]{1,0:T(8,128)(2,1)S(1)} %slice_bitcast_fusion), channel_id=1, source_target_pairs={{0,1},{1,2},{2,3},{3,4},{4,5},{5,6},{6,7},{7,8},{8,9},{9,10},{10,1... | collective-permute-start | bytes 442376 | tf_op jit(solution)/shard_map/ppermute | solution.py:94
  27.0 7.3 %collective-permute-start.1 = (bf16[16,4608]{1,0:T(8,128)(2,1)S(1)}, bf16[16,4608]{1,0:T(8,128)(2,1)S(1)}, u32[]{:S(2)}, u32[]{:S(2)}) collective-permute-start(bf16[16,4608]{1,0:T(8,128)(2,1)S(1)} %collective-permute-done), channel_id=1, source_target_pairs={{0,1},{1,2},{2,3},{3,4},{4,5},{5,6},{6,7},{7,8},{8,9},{9,10},{10,1... | collective-permute-start | bytes 442376 | tf_op jit(solution)/shard_map/ppermute | solution.py:94
  34.2 7.3 %collective-permute-start.2 = (bf16[16,4608]{1,0:T(8,128)(2,1)S(1)}, bf16[16,4608]{1,0:T(8,128)(2,1)S(1)}, u32[]{:S(2)}, u32[]{:S(2)}) collective-permute-start(bf16[16,4608]{1,0:T(8,128)(2,1)S(1)} %collective-permute-done.1), channel_id=1, source_target_pairs={{0,1},{1,2},{2,3},{3,4},{4,5},{5,6},{6,7},{7,8},{8,9},{9,10},{10,1... | collective-permute-start | bytes 442376 | tf_op jit(solution)/shard_map/ppermute | solution.py:94
  41.5 7.3 %collective-permute-start.3 = (bf16[16,4608]{1,0:T(8,128)(2,1)S(1)}, bf16[16,4608]{1,0:T(8,128)(2,1)S(1)}, u32[]{:S(2)}, u32[]{:S(2)}) collective-permute-start(bf16[16,4608]{1,0:T(8,128)(2,1)S(1)} %collective-permute-done.2), channel_id=1, source_target_pairs={{0,1},{1,2},{2,3},{3,4},{4,5},{5,6},{6,7},{7,8},{8,9},{9,10},{10,1... | collective-permute-start | bytes 442376 | tf_op jit(solution)/shard_map/ppermute | solution.py:94
  48.7 7.3 %collective-permute-start.4 = (bf16[16,4608]{1,0:T(8,128)(2,1)S(1)}, bf16[16,4608]{1,0:T(8,128)(2,1)S(1)}, u32[]{:S(2)}, u32[]{:S(2)}) collective-permute-start(bf16[16,4608]{1,0:T(8,128)(2,1)S(1)} %collective-permute-done.3), channel_id=1, source_target_pairs={{0,1},{1,2},{2,3},{3,4},{4,5},{5,6},{6,7},{7,8},{8,9},{9,10},{10,1... | collective-permute-start | bytes 442376 | tf_op jit(solution)/shard_map/ppermute | solution.py:94
  56.0 7.3 %collective-permute-start.5 = (bf16[16,4608]{1,0:T(8,128)(2,1)S(1)}, bf16[16,4608]{1,0:T(8,128)(2,1)S(1)}, u32[]{:S(2)}, u32[]{:S(2)}) collective-permute-start(bf16[16,4608]{1,0:T(8,128)(2,1)S(1)} %collective-permute-done.4), channel_id=1, source_target_pairs={{0,1},{1,2},{2,3},{3,4},{4,5},{5,6},{6,7},{7,8},{8,9},{9,10},{10,1... | collective-permute-start | bytes 442376 | tf_op jit(solution)/shard_map/ppermute | solution.py:94
  63.3 7.3 %collective-permute-start.6 = (bf16[16,4608]{1,0:T(8,128)(2,1)S(1)}, bf16[16,4608]{1,0:T(8,128)(2,1)S(1)}, u32[]{:S(2)}, u32[]{:S(2)}) collective-permute-start(bf16[16,4608]{1,0:T(8,128)(2,1)S(1)} %collective-permute-done.5), channel_id=1, source_target_pairs={{0,1},{1,2},{2,3},{3,4},{4,5},{5,6},{6,7},{7,8},{8,9},{9,10},{10,1... | collective-permute-start | bytes 442376 | tf_op jit(solution)/shard_map/ppermute | solution.py:94
  70.5 7.3 %collective-permute-start.7 = (bf16[16,4608]{1,0:T(8,128)(2,1)S(1)}, bf16[16,4608]{1,0:T(8,128)(2,1)S(1)}, u32[]{:S(2)}, u32[]{:S(2)}) collective-permute-start(bf16[16,4608]{1,0:T(8,128)(2,1)S(1)} %collective-permute-done.6), channel_id=1, source_target_pairs={{0,1},{1,2},{2,3},{3,4},{4,5},{5,6},{6,7},{7,8},{8,9},{9,10},{10,1... | collective-permute-start | bytes 442376 | tf_op jit(solution)/shard_map/ppermute | solution.py:94
  77.8 7.3 %collective-permute-start.8 = (bf16[16,4608]{1,0:T(8,128)(2,1)S(1)}, bf16[16,4608]{1,0:T(8,128)(2,1)S(1)}, u32[]{:S(2)}, u32[]{:S(2)}) collective-permute-start(bf16[16,4608]{1,0:T(8,128)(2,1)S(1)} %collective-permute-done.7), channel_id=1, source_target_pairs={{0,1},{1,2},{2,3},{3,4},{4,5},{5,6},{6,7},{7,8},{8,9},{9,10},{10,1... | collective-permute-start | bytes 442376 | tf_op jit(solution)/shard_map/ppermute | solution.py:94
  85.1 7.3 %collective-permute-start.9 = (bf16[16,4608]{1,0:T(8,128)(2,1)S(1)}, bf16[16,4608]{1,0:T(8,128)(2,1)S(1)}, u32[]{:S(2)}, u32[]{:S(2)}) collective-permute-start(bf16[16,4608]{1,0:T(8,128)(2,1)S(1)} %collective-permute-done.8), channel_id=1, source_target_pairs={{0,1},{1,2},{2,3},{3,4},{4,5},{5,6},{6,7},{7,8},{8,9},{9,10},{10,1... | collective-permute-start | bytes 442376 | tf_op jit(solution)/shard_map/ppermute | solution.py:94
  92.3 7.3 %collective-permute-start.10 = (bf16[16,4608]{1,0:T(8,128)(2,1)S(1)}, bf16[16,4608]{1,0:T(8,128)(2,1)S(1)}, u32[]{:S(2)}, u32[]{:S(2)}) collective-permute-start(bf16[16,4608]{1,0:T(8,128)(2,1)S(1)} %collective-permute-done.9), channel_id=1, source_target_pairs={{0,1},{1,2},{2,3},{3,4},{4,5},{5,6},{6,7},{7,8},{8,9},{9,10},{10,1... | collective-permute-start | bytes 442376 | tf_op jit(solution)/shard_map/ppermute | solution.py:94
  99.6 7.9 %collective-permute-start.11 = (bf16[16,4608]{1,0:T(8,128)(2,1)S(1)}, bf16[16,4608]{1,0:T(8,128)(2,1)S(1)}, u32[]{:S(2)}, u32[]{:S(2)}) collective-permute-start(bf16[16,4608]{1,0:T(8,128)(2,1)S(1)} %collective-permute-done.10), channel_id=1, source_target_pairs={{0,1},{1,2},{2,3},{3,4},{4,5},{5,6},{6,7},{7,8},{8,9},{9,10},{10,1... | collective-permute-start | bytes 442376 | tf_op jit(solution)/shard_map/ppermute | solution.py:94
  100.9 42.7 %all-to-all-start.1 = ((bf16[16,1,1]{2,1,0:T(2,128)(2,1)}), bf16[16,1,1]{2,1,0:T(2,128)(2,1)S(1)}, u32[]{:S(2)}, u32[]{:S(2)}) async-start(bf16[16,1,1]{2,1,0:T(2,128)(2,1)} %broadcast_in_dim.70), calls=%async_computation.1 | async-start | bytes 16384 | tf_op jit(solution)/shard_map/all_to_all | solution.py:79
  106.7 93.4 %reduce-scatter.2.cloned.1.call-start = ((), (), s32[]{:S(2)}) async-start(), calls=%async_computation.3 | async-start | bytes 2506752 | tf_op jit(solution)/shard_map/reduce_scatter | solution.py:128
  107.5 7.3 %collective-permute-start.12 = (bf16[16,4608]{1,0:T(8,128)(2,1)S(1)}, bf16[16,4608]{1,0:T(8,128)(2,1)S(1)}, u32[]{:S(2)}, u32[]{:S(2)}) collective-permute-start(bf16[16,4608]{1,0:T(8,128)(2,1)S(1)} %collective-permute-done.11), channel_id=1, source_target_pairs={{0,1},{1,2},{2,3},{3,4},{4,5},{5,6},{6,7},{7,8},{8,9},{9,10},{10,1... | collective-permute-start | bytes 442376 | tf_op jit(solution)/shard_map/ppermute | solution.py:94
  114.8 7.3 %collective-permute-start.13 = (bf16[16,4608]{1,0:T(8,128)(2,1)S(1)}, bf16[16,4608]{1,0:T(8,128)(2,1)S(1)}, u32[]{:S(2)}, u32[]{:S(2)}) collective-permute-start(bf16[16,4608]{1,0:T(8,128)(2,1)S(1)} %collective-permute-done.12), channel_id=1, source_target_pairs={{0,1},{1,2},{2,3},{3,4},{4,5},{5,6},{6,7},{7,8},{8,9},{9,10},{10,1... | collective-permute-start | bytes 442376 | tf_op jit(solution)/shard_map/ppermute | solution.py:94
  122.1 7.4 %collective-permute-start.14 = (bf16[16,4608]{1,0:T(8,128)(2,1)S(1)}, bf16[16,4608]{1,0:T(8,128)(2,1)}, u32[]{:S(2)}, u32[]{:S(2)}) collective-permute-start(bf16[16,4608]{1,0:T(8,128)(2,1)S(1)} %collective-permute-done.13), channel_id=1, source_target_pairs={{0,1},{1,2},{2,3},{3,4},{4,5},{5,6},{6,7},{7,8},{8,9},{9,10},{10,1... | collective-permute-start | bytes 442376 | tf_op jit(solution)/shard_map/ppermute | solution.py:94
  130.5 2.1 copy-start.3
  130.5 2.1 copy-start.7
  131.9 1.8 copy-start.8
  132.6 2.2 %copy-start.5 = (f32[64]{0:T(128)S(1)}, f32[64]{0:T(128)}, u32[]{:S(2)}) copy-start(f32[64]{0:T(128)} %multiply_power_fusion) | copy-start | bytes 772
  134.8 4.4 %copy-start.6 = (s32[16,1,1]{0,2,1:T(1,128)S(1)}, s32[16,1,1]{0,2,1:T(1,128)}, u32[]{:S(2)}) copy-start(s32[16,1,1]{0,2,1:T(1,128)} %fusion.53) | copy-start | bytes 196
  134.8 5.8 %copy-start.2 = (f32[16,2,4608]{2,1,0:T(2,128)S(1)}, f32[16,2,4608]{2,1,0:T(2,128)}, u32[]{:S(2)}) copy-start(f32[16,2,4608]{2,1,0:T(2,128)} %param.14) | copy-start | bytes 1769476
  134.8 8.7 %copy-start.4 = (f32[1,4608]{1,0:T(1,128)S(1)}, f32[1,4608]{1,0:T(1,128)}, u32[]{:S(2)}) copy-start(f32[1,4608]{1,0:T(1,128)} %param.21) | copy-start | bytes 55300
  135.2 1.3 collective-permute-start.15
  143.6 14.1 %all-to-all-start = ((bf16[16,2,4608]{2,1,0:T(2,128)(2,1)}), bf16[16,2,4608]{2,1,0:T(2,128)(2,1)S(1)}, u32[]{:S(2)}, u32[]{:S(2)}) async-start(bf16[16,2,4608]{2,1,0:T(2,128)(2,1)} %select_convert_fusion), calls=%async_computation | async-start | bytes 589824 | tf_op jit(solution)/shard_map/all_to_all | solution.py:76
Sparse Core Ops, SparseCore 0:
  139.3 60.6 reduce-scatter.1
